TPU v7x, 32 devices: a whole 2x2x4 slice. The times are simulated.
32 devices in a mesh: expert: 2 (over y), tensor: 16 (over z, x, core).
Axes of the slice: x: 2, y: 2, z: 4, core: 2. Of those that a mesh axis runs over, the one named last changes fastest.
Arguments:
- tokens: bfloat16 [256, 6144], P(('expert', 'tensor')), may hold values from -6 to 6
- expert_ids: int32 [256, 2], P(('expert', 'tensor')), may hold values from 0 to 7, all different within a row; in each aligned block of 8 rows (0 to 7, 8 to 15, ...) at most 3 rows name the same one
- gates: float32 [256, 2], P(('expert', 'tensor')), may hold values from 0.2 to 1
- w_gate: bfloat16 [8, 6144, 8192], P('expert', None, 'tensor'), may hold values from -0.078125 to 0.078125
- w_up: bfloat16 [8, 6144, 8192], P('expert', None, 'tensor'), may hold values from -0.078125 to 0.078125
- w_down: bfloat16 [8, 8192, 6144], P('expert', 'tensor'), may hold values from -0.0625 to 0.0625
Outputs:
- mixed: bfloat16 [256, 6144], P(('expert', 'tensor'))
Inputs may be any that keep to these rules, and one draw needn't show every extreme that they name: `expert_ids`: each token names 2 different experts. Among the tokens of one device (aligned blocks of 8 rows) no expert is named more than 3 times, a bound that some expert reaches in every block.
All inputs are finite; a program needn't handle non-finite values.
Results may differ from a plain program's by a relative error of at most 0.02.
Values may be sent and summed in bfloat16 or wider, within the bound.
A program may use at most 128 MiB of HBM per device.

v0:
```python
import jax
import jax.numpy as jnp
from jax import lax
from jax.sharding import PartitionSpec as P

EXPERTS = 8
TOPK = 2
CAP = 3


def route_places(ids):
    flat = ids.reshape(-1)
    onehot = (flat[:, None] == jnp.arange(EXPERTS, dtype=jnp.int32)[None, :]).astype(jnp.int32)
    before = jnp.cumsum(onehot, axis=0) - onehot
    slot = jnp.sum(before * onehot, axis=1)
    return flat * CAP + slot


def body(tokens, expert_ids, gates, w_gate, w_up, w_down):
    n_groups = lax.axis_size("expert")
    local_experts = w_gate.shape[0]
    width = tokens.shape[1]
    tok_count = tokens.shape[0]
    places = route_places(expert_ids)
    picker = (jnp.arange(EXPERTS * CAP, dtype=jnp.int32)[:, None] == places[None, :]).astype(
        jnp.bfloat16
    )
    doubled = jnp.repeat(tokens, TOPK, axis=0)
    buffer = jnp.dot(picker, doubled, preferred_element_type=jnp.float32).astype(jnp.bfloat16)
    buffer = buffer.reshape(n_groups, local_experts * CAP, width)
    arrived = lax.all_to_all(buffer, "expert", split_axis=0, concat_axis=0, tiled=True)
    regrouped = arrived.reshape(n_groups, local_experts, CAP, width).transpose(1, 0, 2, 3)
    regrouped = regrouped.reshape(local_experts, n_groups * CAP, width)
    piece = lax.all_gather(regrouped, "tensor", axis=1, tiled=True)
    gate_act = jnp.einsum("erd,edf->erf", piece, w_gate, preferred_element_type=jnp.float32)
    up_act = jnp.einsum("erd,edf->erf", piece, w_up, preferred_element_type=jnp.float32)
    hidden = (jax.nn.silu(gate_act) * up_act).astype(jnp.bfloat16)
    piece = hidden
    term = jnp.einsum("erf,efd->red", piece, w_down, preferred_element_type=jnp.float32)
    summed = lax.psum_scatter(
        term.reshape(n_groups * CAP * lax.axis_size("tensor"), local_experts * width).astype(
            jnp.bfloat16
        ),
        "tensor",
        scatter_dimension=0,
        tiled=True,
    )
    results = summed.reshape(n_groups, CAP, local_experts, width)
    returned = lax.all_to_all(results, "expert", split_axis=0, concat_axis=0, tiled=True)
    results_flat = returned.transpose(0, 2, 1, 3).reshape(EXPERTS * CAP, width)
    weights = (jnp.arange(EXPERTS * CAP, dtype=jnp.int32)[None, :] == places[:, None]).astype(
        jnp.float32
    )
    weights = weights * gates.reshape(-1)[:, None]
    weights = jnp.sum(weights.reshape(tok_count, TOPK, EXPERTS * CAP), axis=1)
    mixed = jnp.dot(weights, results_flat.astype(jnp.float32), precision=lax.Precision.HIGHEST)
    return mixed.astype(jnp.bfloat16)


def solution(mesh):
    return jax.shard_map(
        body,
        mesh=mesh,
        in_specs=(
            P(("expert", "tensor"), None),
            P(("expert", "tensor"), None),
            P(("expert", "tensor"), None),
            P("expert", None, "tensor"),
            P("expert", None, "tensor"),
            P("expert", "tensor", None),
        ),
        out_specs=P(("expert", "tensor"), None),
        check_vma=False,
    )
```

profile of v0, /device:TPU:19, one launch (start us, length us, event | category | flops | bytes accessed | tf_op | source)
XLA Modules:
  0.0 246.6 jit_solution(2106851167836730849)
XLA Ops:
  6.5 0.0 all-gather.2.cloned.1.call-start
  6.5 0.8 copy.28
  7.3 0.1 eq.43
  7.4 0.1 fusion.12
  7.5 0.2 select_reduce_fusion.1
  7.7 1.0 broadcast_in_dim.2
  8.7 0.1 reshape.53
  8.8 0.2 convolution_convert_fusion.1
  9.0 0.1 reshape.54
  9.1 8.2 %all_to_all.10 = bf16[2,12,6144]{2,1,0:T(8,128)(2,1)S(1)} all-to-all(bf16[2,12,6144]{2,1,0:T(8,128)(2,1)S(1)} %reshape.54), channel_id=1, replica_groups=mesh['expert'=2,'tensor'=16] {'expert'}, dimensions={0} | all-to-all | bytes 589824 | tf_op jit(solution)/shard_map/all_to_all | solution.py:31
  17.3 0.3 copy.31
  17.6 0.9 copy.32
  18.5 0.0 all-gather.2.cloned.1.call-update
  18.5 53.3 %all-gather.2.cloned.1.call-done = bf16[4,96,6144]{2,0,1:T(4,128)(2,1)} async-done(((bf16[4,6,6144]{2,0,1:T(4,128)(2,1)}), bf16[4,96,6144]{2,0,1:T(4,128)(2,1)}) %all-gather.2.cloned.1.call-update) | async-done | bytes 4718608 | tf_op jit(solution)/shard_map/all_gather | solution.py:34
  71.8 0.0 copy-start
  71.8 14.0 %fusion.4 = f32[4,96,512]{2,1,0:T(8,128)S(1)} fusion(bf16[4,6144,512]{2,1,0:T(8,128)(2,1)} %param.9, bf16[4,96,6144]{2,0,1:T(4,128)(2,1)} %all-gather.2.cloned.1.call-done), kind=kOutput, calls=%fused_computation.6 | convolution fusion | flops 2415919104 | bytes 30670848 | tf_op jit(solution)/shard_map/erd,edf->erf/dot_general | solution.py:35
  85.9 0.0 copy-done
  85.9 15.0 %fusion.9 = bf16[4,96,512]{2,1,0:T(8,128)(2,1)S(1)} fusion(bf16[4,6144,512]{2,1,0:T(8,128)(2,1)} %param.10, bf16[4,96,6144]{2,0,1:T(4,128)(2,1)S(1)} %copy-done, f32[4,96,512]{2,1,0:T(8,128)S(1)} %fusion.4), kind=kOutput, calls=%fused_computation.9 | convolution fusion | flops 2417098752 | bytes 31064064 | tf_op jit(solution)/shard_map/erd,edf->erf/dot_general | solution.py:36
  100.8 12.5 %fusion.1 = bf16[4,12,8,6144]{3,2,1,0:T(8,128)(2,1)S(1)} fusion(bf16[4,96,512]{2,1,0:T(8,128)(2,1)S(1)} %fusion.9, bf16[4,512,6144]{2,1,0:T(8,128)(2,1)} %param.11), kind=kOutput, calls=%fused_computation.1 | convolution fusion | flops 2418278400 | bytes 30277632 | tf_op jit(solution)/shard_map/erf,efd->red/dot_general | solution.py:39
  113.3 0.0 copy-start.3
  113.3 2.6 %copy.37 = bf16[4,12,8,6144]{3,2,0,1:T(8,128)(2,1)} copy(bf16[4,12,8,6144]{3,2,1,0:T(8,128)(2,1)S(1)} %fusion.1) | data formatting | bytes 9437184 | tf_op jit(solution)/shard_map/convert_element_type | solution.py:41
  116.0 0.0 copy-start.2
  116.0 69.9 %fusion = bf16[8,24576]{1,0:T(8,128)(2,1)S(1)} fusion(bf16[96,24576]{1,0:T(8,128)(2,1)} %bitcast.19), kind=kCustom, calls=%all-reduce-scatter | all-reduce-scatter fusion | flops 3145729 | bytes 5112320
  185.8 6.1 %collective-permute-start.2 = (bf16[8,24576]{1,0:T(8,128)(2,1)S(1)}, bf16[8,24576]{1,0:T(8,128)(2,1)S(1)}, u32[]{:S(2)}, u32[]{:S(2)}) collective-permute-start(bf16[8,24576]{1,0:T(8,128)(2,1)S(1)} %fusion), channel_id=1, source_target_pairs={{0,3},{1,4},{2,5},{3,6},{4,7},{5,8},{6,9},{7,10},{8,11},{9,12},{10... | collective-permute-start | bytes 1179656
  192.0 1.9 collective-permute-start.1
  193.9 2.7 %collective-permute-start = (bf16[8,24576]{1,0:T(8,128)(2,1)S(1)}, bf16[8,24576]{1,0:T(8,128)(2,1)S(1)}, u32[]{:S(2)}, u32[]{:S(2)}) collective-permute-start(bf16[8,24576]{1,0:T(8,128)(2,1)S(1)} %fusion), channel_id=1, source_target_pairs={{0,1},{1,2},{2,3},{3,4},{4,5},{5,6},{6,7},{7,8},{8,9},{9,10},{10,1... | collective-permute-start | bytes 1179656
  196.6 0.1 slice
  196.7 1.9 collective-permute-start.3
  198.7 0.1 reduce_sum.21
  198.8 0.0 copy-done.3
  198.8 0.6 dynamic-slice.4
  200.0 22.6 %collective-permute-done.3 = bf16[6,24576]{1,0:T(8,128)(2,1)S(1)} collective-permute-done((bf16[6,24576]{1,0:T(8,128)(2,1)S(1)}, bf16[6,24576]{1,0:T(8,128)(2,1)S(1)}, u32[]{:S(2)}, u32[]{:S(2)}) %collective-permute-start.3) | collective-permute-done | bytes 294944
  222.6 0.0 copy-start.1
  222.6 0.0 collective-permute-done.2
  222.6 0.0 collective-permute-done.1
  222.6 0.7 copy-done.1
  223.3 0.0 collective-permute-done
  223.3 6.1 %concatenate = bf16[38,24576]{1,0:T(8,128)(2,1)S(1)} concatenate(bf16[6,24576]{1,0:T(8,128)(2,1)} %copy-done.1, bf16[8,24576]{1,0:T(8,128)(2,1)S(1)} %collective-permute-done.2, bf16[8,24576]{1,0:T(8,128)(2,1)S(1)} %collective-permute-done.1, bf16[8,24576]{1,0:T(8,128)(2,1)S(1)} %collective-permute-done, bf16[8,24576]{1,0:T(8,128)(2,1)S(1)} %fusion), dimensions={0} | concatenate | bytes 3735552
  229.4 0.1 constant_dynamic-slice_fusion
  229.6 1.1 reshape.57
  230.7 3.4 %all-to-all-start.1 = ((bf16[2,3,4,6144]{3,2,1,0:T(4,128)(2,1)}), bf16[2,3,4,6144]{3,2,1,0:T(4,128)(2,1)S(1)}, u32[]{:S(2)}, u32[]{:S(2)}) async-start(bf16[2,3,4,6144]{3,2,1,0:T(4,128)(2,1)} %reshape.57), calls=%async_computation.1 | async-start | bytes 589824 | tf_op jit(solution)/shard_map/all_to_all | solution.py:49
  234.2 0.1 copy.30
  234.2 0.0 copy-done.2
  234.2 0.1 select_reduce_fusion
  234.3 4.0 %all-to-all-done.1 = bf16[2,3,4,6144]{3,2,1,0:T(4,128)(2,1)S(1)} async-done(((bf16[2,3,4,6144]{3,2,1,0:T(4,128)(2,1)}), bf16[2,3,4,6144]{3,2,1,0:T(4,128)(2,1)S(1)}, u32[]{:S(2)}, u32[]{:S(2)}) %all-to-all-start.1) | async-done | bytes 294944 | tf_op jit(solution)/shard_map/all_to_all | solution.py:49
  238.3 0.3 copy.36
  238.6 0.3 reshape.58
  238.8 0.9 convolution_convert_fusion.2
  (3 shorter events, 0.0 us)
Async XLA Ops:
  6.5 65.3 %all-gather.2.cloned.1.call-start = ((), (), s32[]{:S(2)}) async-start(), calls=%async_computation.2 | async-start | bytes 5013504 | tf_op jit(solution)/shard_map/all_gather | solution.py:34
  71.8 14.0 %copy-start = (bf16[4,96,6144]{2,0,1:T(4,128)(2,1)S(1)}, bf16[4,96,6144]{2,0,1:T(4,128)(2,1)}, u32[]{:S(2)}) copy-start(bf16[4,96,6144]{2,0,1:T(4,128)(2,1)} %all-gather.2.cloned.1.call-done) | copy-start | bytes 14155780
  113.3 85.4 %copy-start.3 = (u32[32]{0:T(128)S(1)}, u32[32]{0:T(128)}, u32[]{:S(2)}) copy-start(u32[32]{0:T(128)} %constant.19) | copy-start | bytes 388
  116.0 118.3 %copy-start.2 = (f32[8,2]{0,1:T(2,128)S(1)}, f32[8,2]{0,1:T(2,128)}, u32[]{:S(2)}) copy-start(f32[8,2]{0,1:T(2,128)} %param.8) | copy-start | bytes 196
  185.8 36.7 %collective-permute-start.2 = (bf16[8,24576]{1,0:T(8,128)(2,1)S(1)}, bf16[8,24576]{1,0:T(8,128)(2,1)S(1)}, u32[]{:S(2)}, u32[]{:S(2)}) collective-permute-start(bf16[8,24576]{1,0:T(8,128)(2,1)S(1)} %fusion), channel_id=1, source_target_pairs={{0,3},{1,4},{2,5},{3,6},{4,7},{5,8},{6,9},{7,10},{8,11},{9,12},{10... | collective-permute-start | bytes 1179656
  192.0 30.6 %collective-permute-start.1 = (bf16[8,24576]{1,0:T(8,128)(2,1)S(1)}, bf16[8,24576]{1,0:T(8,128)(2,1)S(1)}, u32[]{:S(2)}, u32[]{:S(2)}) collective-permute-start(bf16[8,24576]{1,0:T(8,128)(2,1)S(1)} %fusion), channel_id=1, source_target_pairs={{0,2},{1,3},{2,4},{3,5},{4,6},{5,7},{6,8},{7,9},{8,10},{9,11},{10,... | collective-permute-start | bytes 1179656
  193.9 29.4 %collective-permute-start = (bf16[8,24576]{1,0:T(8,128)(2,1)S(1)}, bf16[8,24576]{1,0:T(8,128)(2,1)S(1)}, u32[]{:S(2)}, u32[]{:S(2)}) collective-permute-start(bf16[8,24576]{1,0:T(8,128)(2,1)S(1)} %fusion), channel_id=1, source_target_pairs={{0,1},{1,2},{2,3},{3,4},{4,5},{5,6},{6,7},{7,8},{8,9},{9,10},{10,1... | collective-permute-start | bytes 1179656
  196.7 25.8 %collective-permute-start.3 = (bf16[6,24576]{1,0:T(8,128)(2,1)S(1)}, bf16[6,24576]{1,0:T(8,128)(2,1)S(1)}, u32[]{:S(2)}, u32[]{:S(2)}) collective-permute-start(bf16[6,24576]{1,0:T(8,128)(2,1)S(1)} %slice), channel_id=1, source_target_pairs={{0,4},{1,5},{2,6},{3,7},{4,8},{5,9},{6,10},{7,11},{8,12},{9,13},{1... | collective-permute-start | bytes 884744
  222.6 0.7 copy-start.1
  230.7 7.6 %all-to-all-start.1 = ((bf16[2,3,4,6144]{3,2,1,0:T(4,128)(2,1)}), bf16[2,3,4,6144]{3,2,1,0:T(4,128)(2,1)S(1)}, u32[]{:S(2)}, u32[]{:S(2)}) async-start(bf16[2,3,4,6144]{3,2,1,0:T(4,128)(2,1)} %reshape.57), calls=%async_computation.1 | async-start | bytes 589824 | tf_op jit(solution)/shard_map/all_to_all | solution.py:49
Sparse Core Ops, SparseCore 0:
  18.6 53.1 all-gather.1
where the time goes:
time: 247 us
  waiting for transfers between devices  79.9 us (32%)
  blocking collectives  78.1 us (32%)
  matrix products  42.6 us (17%)
  starting transfers between devices  16.1 us (7%)
  local copies, waits for them, and re-layouts  15.3 us (6%)
  between operations  14.2 us (6%)
    unnamed x1, blocking collectives  69.9 us
    all_gather x1, waiting for transfers between devices, body(): piece = lax.all_gather(regrouped, 'tensor', axis=1, tiled=True)  53.3 us
    unnamed x5, waiting for transfers between devices  22.6 us
    dot_general x1, matrix products, body(): jnp.einsum('erd,edf->erf', piece, w_up, preferred_element_type=jnp.float32)  15 us
    dot_general x1, matrix products, body(): jnp.einsum('erd,edf->erf', piece, w_gate, preferred_element_type=jnp.floa...  14 us
    unnamed x4, starting transfers between devices  12.7 us
    dot_general x1, matrix products, body(): jnp.einsum('erf,efd->red', piece, w_down, preferred_element_type=jnp.floa...  12.5 us
    unnamed x13, local copies, waits for them, and re-layouts  8.41 us
  transfers between devices with their start and end apart: 6, of which 3 were waited for; matrix products, arithmetic and copies ran while one was open for 0% of the time, Pallas kernels for 0%

commit v1 on v0

--- a/solution.py
+++ b/solution.py
@@ -31,7 +31,9 @@
     arrived = lax.all_to_all(buffer, "expert", split_axis=0, concat_axis=0, tiled=True)
     regrouped = arrived.reshape(n_groups, local_experts, CAP, width).transpose(1, 0, 2, 3)
     regrouped = regrouped.reshape(local_experts, n_groups * CAP, width)
-    piece = lax.all_gather(regrouped, "tensor", axis=1, tiled=True)
+    piece = jnp.concatenate(
+        lax.all_to_all(jnp.stack([regrouped] * lax.axis_size("tensor")), "tensor", 0, 0), axis=1
+    )
     gate_act = jnp.einsum("erd,edf->erf", piece, w_gate, preferred_element_type=jnp.float32)
     up_act = jnp.einsum("erd,edf->erf", piece, w_up, preferred_element_type=jnp.float32)
     hidden = (jax.nn.silu(gate_act) * up_act).astype(jnp.bfloat16)

time: 247 us -> 290 us (1.17)
  blocking collectives: 78.1 us -> 188 us
  waiting for transfers between devices: 79.9 us -> 26.4 us
  between operations: 14.2 us -> 0.82 us
    all_to_all x0 -> x1, blocking collectives: none -> 109 us  [body(): lax.all_to_all(jnp.stack([regrouped] * lax.axis_size('tensor')), 'tensor'...]
    all_gather x1 -> x0, waiting for transfers between devices: 53.3 us -> none  [body(): piece = lax.all_gather(regrouped, 'tensor', axis=1, tiled=True)]
    unnamed x5 -> x4, waiting for transfers between devices: 22.6 us -> 22.4 us
    unnamed x13 -> x11, local copies, waits for them, and re-layouts: 8.41 us -> 8.4 us
  transfers between devices with their start and end apart: 6 -> 5, of which waited for: 3 -> 2; matrix products, arithmetic and copies ran while one was open for 0% -> 0% of each run, Pallas kernels for 0% -> 0%
where the time goes in v1:
time: 290 us; the launch traced here: 289 us
  blocking collectives  188 us (65%)
  matrix products  40.4 us (14%)
  waiting for transfers between devices  26.4 us (9%)
  local copies, waits for them, and re-layouts  16.9 us (6%)
  starting transfers between devices  16.3 us (6%)
    all_to_all x1, blocking collectives, body(): lax.all_to_all(jnp.stack([regrouped] * lax.axis_size('tensor')), 'tensor'...  109 us
    unnamed x1, blocking collectives  70.5 us
    unnamed x4, waiting for transfers between devices  22.4 us
    dot_general x1, matrix products, body(): jnp.einsum('erd,edf->erf', piece, w_up, preferred_element_type=jnp.float32)  15 us
    unnamed x4, starting transfers between devices  12.8 us
    dot_general x1, matrix products, body(): jnp.einsum('erf,efd->red', piece, w_down, preferred_element_type=jnp.floa...  12.5 us
    dot_general x1, matrix products, body(): jnp.einsum('erd,edf->erf', piece, w_gate, preferred_element_type=jnp.floa...  11.8 us
    unnamed x11, local copies, waits for them, and re-layouts  8.4 us
  transfers between devices with their start and end apart: 5, of which 2 were waited for; matrix products, arithmetic and copies ran while one was open for 0% of the time, Pallas kernels for 0%

profile of v1, /device:TPU:19, one launch (start us, length us, event | category | flops | bytes accessed | tf_op | source)
XLA Modules:
  0.0 289.3 jit_solution(2380274594425487655)
XLA Ops:
  0.0 0.8 copy.27
  0.8 0.1 eq.43
  0.8 0.1 fusion.12
  0.9 0.2 select_reduce_fusion.1
  1.1 1.0 broadcast_in_dim.2
  2.1 0.1 reshape.58
  2.2 0.2 convolution_convert_fusion.1
  2.5 0.1 reshape.59
  2.5 8.2 %all_to_all.15 = bf16[2,12,6144]{2,1,0:T(8,128)(2,1)S(1)} all-to-all(bf16[2,12,6144]{2,1,0:T(8,128)(2,1)S(1)} %reshape.59), channel_id=1, replica_groups=mesh['expert'=2,'tensor'=16] {'expert'}, dimensions={0} | all-to-all | bytes 589824 | tf_op jit(solution)/shard_map/all_to_all | solution.py:31
  10.7 0.3 copy.30
  11.1 0.2 copy.31
  11.2 2.3 stack.3
  13.6 109.4 %all_to_all.16 = bf16[16,4,6,6144]{3,1,2,0:T(4,128)(2,1)S(1)} all-to-all(bf16[16,4,6,6144]{3,1,2,0:T(4,128)(2,1)S(1)} %stack.3), channel_id=1, replica_groups=mesh['expert'=2,'tensor'=16] {'tensor'}, dimensions={0} | all-to-all | bytes 9437184 | tf_op jit(solution)/shard_map/all_to_all | solution.py:35
  122.9 11.8 %fusion.4 = f32[4,96,512]{2,1,0:T(8,128)S(1)} fusion(bf16[4,6144,512]{2,1,0:T(8,128)(2,1)} %param.9, bf16[4,96,6144]{2,0,1:T(4,128)(2,1)S(1)} %bitcast.22), kind=kOutput, calls=%fused_computation.6 | convolution fusion | flops 2415919104 | bytes 30670848 | tf_op jit(solution)/shard_map/erd,edf->erf/dot_general | solution.py:37
  134.8 15.0 %fusion.9 = bf16[4,96,512]{2,1,0:T(8,128)(2,1)S(1)} fusion(bf16[4,6144,512]{2,1,0:T(8,128)(2,1)} %param.10, bf16[4,96,6144]{2,0,1:T(4,128)(2,1)S(1)} %bitcast.23, f32[4,96,512]{2,1,0:T(8,128)S(1)} %fusion.4), kind=kOutput, calls=%fused_computation.9 | convolution fusion | flops 2417098752 | bytes 31064064 | tf_op jit(solution)/shard_map/erd,edf->erf/dot_general | solution.py:38
  149.7 12.5 %fusion.1 = bf16[4,12,8,6144]{3,2,1,0:T(8,128)(2,1)S(1)} fusion(bf16[4,96,512]{2,1,0:T(8,128)(2,1)S(1)} %fusion.9, bf16[4,512,6144]{2,1,0:T(8,128)(2,1)} %param.11), kind=kOutput, calls=%fused_computation.1 | convolution fusion | flops 2418278400 | bytes 30277632 | tf_op jit(solution)/shard_map/erf,efd->red/dot_general | solution.py:41
  162.2 2.7 copy.36
  164.9 0.0 copy-start.2
  164.9 0.0 copy-start.1
  164.9 70.5 %fusion = bf16[8,24576]{1,0:T(8,128)(2,1)S(1)} fusion(bf16[96,24576]{1,0:T(8,128)(2,1)} %bitcast.24), kind=kCustom, calls=%all-reduce-scatter | all-reduce-scatter fusion | flops 3145729 | bytes 5112320
  235.4 6.3 %collective-permute-start.2 = (bf16[8,24576]{1,0:T(8,128)(2,1)S(1)}, bf16[8,24576]{1,0:T(8,128)(2,1)S(1)}, u32[]{:S(2)}, u32[]{:S(2)}) collective-permute-start(bf16[8,24576]{1,0:T(8,128)(2,1)S(1)} %fusion), channel_id=1, source_target_pairs={{0,3},{1,4},{2,5},{3,6},{4,7},{5,8},{6,9},{7,10},{8,11},{9,12},{10... | collective-permute-start | bytes 1179656
  241.7 1.9 collective-permute-start.1
  243.6 2.7 collective-permute-start
  246.4 0.1 slice
  246.5 1.9 collective-permute-start.3
  248.4 0.1 reduce_sum.21
  248.5 0.0 copy-done.2
  248.5 0.6 dynamic-slice.4
  249.7 22.4 %collective-permute-done.3 = bf16[6,24576]{1,0:T(8,128)(2,1)S(1)} collective-permute-done((bf16[6,24576]{1,0:T(8,128)(2,1)S(1)}, bf16[6,24576]{1,0:T(8,128)(2,1)S(1)}, u32[]{:S(2)}, u32[]{:S(2)}) %collective-permute-start.3) | collective-permute-done | bytes 294944
  272.1 0.0 copy-start
  272.1 0.0 collective-permute-done.2
  272.1 0.0 collective-permute-done.1
  272.1 0.7 copy-done
  272.9 0.0 collective-permute-done
  272.9 6.1 %concatenate = bf16[38,24576]{1,0:T(8,128)(2,1)S(1)} concatenate(bf16[6,24576]{1,0:T(8,128)(2,1)} %copy-done, bf16[8,24576]{1,0:T(8,128)(2,1)S(1)} %collective-permute-done.2, bf16[8,24576]{1,0:T(8,128)(2,1)S(1)} %collective-permute-done.1, bf16[8,24576]{1,0:T(8,128)(2,1)S(1)} %collective-permute-done, bf16[8,24576]{1,0:T(8,128)(2,1)S(1)} %fusion), dimensions={0} | concatenate | bytes 3735552
  279.0 0.1 constant_dynamic-slice_fusion
  279.1 1.1 reshape.63
  280.2 3.4 %all-to-all-start.2 = ((bf16[2,3,4,6144]{3,2,1,0:T(4,128)(2,1)}), bf16[2,3,4,6144]{3,2,1,0:T(4,128)(2,1)S(1)}, u32[]{:S(2)}, u32[]{:S(2)}) async-start(bf16[2,3,4,6144]{3,2,1,0:T(4,128)(2,1)} %reshape.63), calls=%async_computation.2 | async-start | bytes 589824 | tf_op jit(solution)/shard_map/all_to_all | solution.py:51
  283.7 0.1 copy.29
  283.8 0.0 copy-done.1
  283.8 0.1 select_reduce_fusion
  283.9 4.0 %all-to-all-done.2 = bf16[2,3,4,6144]{3,2,1,0:T(4,128)(2,1)S(1)} async-done(((bf16[2,3,4,6144]{3,2,1,0:T(4,128)(2,1)}), bf16[2,3,4,6144]{3,2,1,0:T(4,128)(2,1)S(1)}, u32[]{:S(2)}, u32[]{:S(2)}) %all-to-all-start.2) | async-done | bytes 294944 | tf_op jit(solution)/shard_map/all_to_all | solution.py:51
  287.9 0.3 copy.35
  288.1 0.3 reshape.64
  288.4 0.9 convolution_convert_fusion.2
  (3 shorter events, 0.0 us)
Async XLA Ops:
  164.9 83.6 %copy-start.2 = (u32[32]{0:T(128)S(1)}, u32[32]{0:T(128)}, u32[]{:S(2)}) copy-start(u32[32]{0:T(128)} %constant.19) | copy-start | bytes 388
  164.9 118.9 %copy-start.1 = (f32[8,2]{0,1:T(2,128)S(1)}, f32[8,2]{0,1:T(2,128)}, u32[]{:S(2)}) copy-start(f32[8,2]{0,1:T(2,128)} %param.8) | copy-start | bytes 196
  235.4 36.7 %collective-permute-start.2 = (bf16[8,24576]{1,0:T(8,128)(2,1)S(1)}, bf16[8,24576]{1,0:T(8,128)(2,1)S(1)}, u32[]{:S(2)}, u32[]{:S(2)}) collective-permute-start(bf16[8,24576]{1,0:T(8,128)(2,1)S(1)} %fusion), channel_id=1, source_target_pairs={{0,3},{1,4},{2,5},{3,6},{4,7},{5,8},{6,9},{7,10},{8,11},{9,12},{10... | collective-permute-start | bytes 1179656
  241.7 30.4 %collective-permute-start.1 = (bf16[8,24576]{1,0:T(8,128)(2,1)S(1)}, bf16[8,24576]{1,0:T(8,128)(2,1)S(1)}, u32[]{:S(2)}, u32[]{:S(2)}) collective-permute-start(bf16[8,24576]{1,0:T(8,128)(2,1)S(1)} %fusion), channel_id=1, source_target_pairs={{0,2},{1,3},{2,4},{3,5},{4,6},{5,7},{6,8},{7,9},{8,10},{9,11},{10,... | collective-permute-start | bytes 1179656
  243.6 29.3 %collective-permute-start = (bf16[8,24576]{1,0:T(8,128)(2,1)S(1)}, bf16[8,24576]{1,0:T(8,128)(2,1)S(1)}, u32[]{:S(2)}, u32[]{:S(2)}) collective-permute-start(bf16[8,24576]{1,0:T(8,128)(2,1)S(1)} %fusion), channel_id=1, source_target_pairs={{0,1},{1,2},{2,3},{3,4},{4,5},{5,6},{6,7},{7,8},{8,9},{9,10},{10,1... | collective-permute-start | bytes 1179656
  246.5 25.7 %collective-permute-start.3 = (bf16[6,24576]{1,0:T(8,128)(2,1)S(1)}, bf16[6,24576]{1,0:T(8,128)(2,1)S(1)}, u32[]{:S(2)}, u32[]{:S(2)}) collective-permute-start(bf16[6,24576]{1,0:T(8,128)(2,1)S(1)} %slice), channel_id=1, source_target_pairs={{0,4},{1,5},{2,6},{3,7},{4,8},{5,9},{6,10},{7,11},{8,12},{9,13},{1... | collective-permute-start | bytes 884744
  272.1 0.7 copy-start
  280.2 7.6 %all-to-all-start.2 = ((bf16[2,3,4,6144]{3,2,1,0:T(4,128)(2,1)}), bf16[2,3,4,6144]{3,2,1,0:T(4,128)(2,1)S(1)}, u32[]{:S(2)}, u32[]{:S(2)}) async-start(bf16[2,3,4,6144]{3,2,1,0:T(4,128)(2,1)} %reshape.63), calls=%async_computation.2 | async-start | bytes 589824 | tf_op jit(solution)/shard_map/all_to_all | solution.py:51
